TPU v7x, 256 devices: a whole 4x4x8 slice. The times are simulated.
256 devices in a mesh: dp: 16 (over y_hi, z), layer: 16 (over x, y_lo, core).
Axes of the slice: x: 4, y: 4 (y_hi: 2, y_lo: 2; y = y_hi * 2 + y_lo), z: 8, core: 2. Of those that a mesh axis runs over, the one named last changes fastest.
Arguments:
- acts: bfloat16 [16, 32, 128, 4096], P('layer', 'dp'), may hold values from -60 to 60
- grads: bfloat16 [16, 32, 128, 14336], P('layer', 'dp'), may hold values from -60 to 60
- proj_in: bfloat16 [16, 64, 4096], P('layer'), may hold values from -0.09375 to 0.09375
- proj_out: bfloat16 [16, 64, 14336], P('layer'), may hold values from -0.046875 to 0.046875
- query_grads: bfloat16 [16, 1024, 4096], P('layer', 'dp'), may hold values from -6 to 6
Outputs:
- scores: float32 [32, 1024], P('dp', 'layer')
All inputs are finite; a program needn't handle non-finite values.
Results may differ from a plain program's by a relative error of at most 0.004.
Values may be sent and summed in bfloat16 or wider, within the bound.
A program may use at most 64 MiB of HBM per device.

v0:
```python
import jax
import jax.numpy as jnp
from jax import lax
from jax.sharding import PartitionSpec as P


def sent_to_all(value, axis):
    size = lax.axis_size(axis)
    return lax.all_to_all(
        jnp.broadcast_to(value[None], (size, *value.shape)), axis, 0, 0, tiled=True
    )


def over_copies(value, axis):
    return sent_to_all(value, axis).sum(axis=0)


def in_one(arrays, axis):
    ends = [0]
    for a in arrays:
        ends.append(ends[-1] + a.size)
    total = over_copies(jnp.concatenate([a.ravel() for a in arrays]), axis)
    return tuple((total[b:e].reshape(a.shape) for a, b, e in zip(arrays, ends, ends[1:])))


def in_order(tiles, dim):
    shape = list(tiles.shape[1:])
    shape[dim] *= tiles.shape[0]
    return jnp.moveaxis(tiles, 0, dim).reshape(shape)


def collect(value, axis, dim):
    return in_order(sent_to_all(value, axis), dim)


def cut_along(value, dim, size):
    shape = value.shape
    tiles = value.reshape(*shape[:dim], size, shape[dim] // size, *shape[dim + 1 :])
    return jnp.moveaxis(tiles, dim, 0)


def summed_on_arrival(value, axis, dim):
    size = lax.axis_size(axis)
    tiles = lax.all_to_all(cut_along(value, dim, size), axis, 0, 0, tiled=True)
    return jnp.sum(tiles, axis=0)


def precondition(grad, cov_in, cov_out):
    size = cov_in.shape[0]
    identity = jnp.eye(size, dtype=jnp.float32)
    damp_in = 0.1 * jnp.trace(cov_in) / size
    damp_out = 0.1 * jnp.trace(cov_out) / size
    factor_in = jnp.linalg.cholesky(cov_in + damp_in * identity)
    factor_out = jnp.linalg.cholesky(cov_out + damp_out * identity)
    batch, outer, inner = grad.shape
    left_side = grad.transpose(1, 0, 2).reshape(outer, batch * inner)
    left_side = jax.scipy.linalg.cho_solve((factor_out, True), left_side)
    right_side = (
        left_side.reshape(outer, batch, inner).transpose(2, 1, 0).reshape(inner, batch * outer)
    )
    right_side = jax.scipy.linalg.cho_solve((factor_in, True), right_side)
    return right_side.reshape(inner, batch, outer).transpose(1, 2, 0)


def local(acts, grads, proj_in, proj_out, query_grads):
    highest = lax.Precision.HIGHEST
    layer_count, examples, length = (acts.shape[0], acts.shape[1], acts.shape[2])
    proj_acts = jnp.einsum("lesd,lrd->lesr", acts, proj_in, preferred_element_type=jnp.float32)
    proj_grads = jnp.einsum("lesd,lrd->lesr", grads, proj_out, preferred_element_type=jnp.float32)
    local_in = jnp.einsum("lesr,lesq->lrq", proj_acts, proj_acts, precision=highest)
    local_out = jnp.einsum("lesr,lesq->lrq", proj_grads, proj_grads, precision=highest)
    cov_in, cov_out = in_one((local_in, local_out), "dp")
    tokens = examples * length * lax.axis_size("dp")
    grad = jnp.einsum("leso,lesi->leoi", proj_grads, proj_acts, precision=highest)
    conditioned = jax.vmap(precondition)(grad, cov_in / tokens, cov_out / tokens)
    conditioned = conditioned.reshape(layer_count, examples, -1).astype(jnp.bfloat16)
    every_corpus = collect(conditioned, "dp", 1)
    local_scores = jnp.einsum(
        "lek,lqk->eq", every_corpus, query_grads, preferred_element_type=jnp.float32
    )
    partial_scores = lax.all_to_all(local_scores, "dp", split_axis=0, concat_axis=1, tiled=True)
    summed = summed_on_arrival(partial_scores, "layer", 1)
    width = conditioned.shape[2]
    layers_all = layer_count * lax.axis_size("layer")
    return summed / jnp.sqrt(jnp.float32(width * layers_all * length))


def solution(mesh):
    return jax.shard_map(
        local,
        mesh=mesh,
        in_specs=(
            P("layer", "dp", None, None),
            P("layer", "dp", None, None),
            P("layer", None, None),
            P("layer", None, None),
            P("layer", "dp", None),
        ),
        out_specs=P("dp", "layer"),
        check_vma=False,
    )
```

profile of v0, /device:TPU:2, one launch (start us, length us, event | category | flops | bytes accessed | tf_op | source)
XLA Modules:
  0.0 108.9 jit_solution(4114973910298127219)
XLA Ops:
  0.0 0.0 copy-start
  0.0 0.0 copy-start.2
  0.0 6.1 %fusion = f32[2,128,64]{1,2,0:T(8,128)S(1)} fusion(bf16[1,2,128,14336]{3,2,1,0:T(8,128)(2,1)} %param.9, bf16[1,64,14336]{2,1,0:T(8,128)(2,1)} %param.11), kind=kOutput, calls=%fused_computation | convolution fusion | flops 469762048 | bytes 9240576 | tf_op jit(solution)/shard_map/lesd,lrd->lesr/dot_general | solution.py:69
  6.1 0.2 convolution_bitcast_fusion.3
  6.3 0.1 reshape.197
  6.4 0.0 copy-done
  6.4 0.0 copy-done.2
  6.4 0.8 fusion.2
  7.1 0.2 convolution_bitcast_fusion.4
  7.4 0.1 reshape.194
  7.4 1.2 %broadcast_in_dim.19 = f32[16,1,8192]{2,1,0:T(1,128)} broadcast(f32[8192]{0:T(1024)S(1)} %pad_maximum_fusion), dimensions={2} | broadcast | bytes 557056 | tf_op jit(solution)/shard_map/broadcast_in_dim | solution.py:10
  8.6 0.0 copy-start.1
  8.6 11.3 %all-to-all-start = ((f32[16,1,8192]{2,1,0:T(1,128)}), f32[16,1,8192]{2,1,0:T(1,128)S(1)}, u32[]{:S(2)}, u32[]{:S(2)}) async-start(f32[16,1,8192]{2,1,0:T(1,128)} %broadcast_in_dim.19), calls=%async_computation | async-start | bytes 1048576 | tf_op jit(solution)/shard_map/all_to_all | solution.py:9
  20.0 0.2 convolution_bitcast_fusion
  20.2 0.1 copy.46
  20.3 0.1 reshape.205
  20.4 16.8 %all-to-all-done = f32[16,1,8192]{2,1,0:T(1,128)S(1)} async-done(((f32[16,1,8192]{2,1,0:T(1,128)}), f32[16,1,8192]{2,1,0:T(1,128)S(1)}, u32[]{:S(2)}, u32[]{:S(2)}) %all-to-all-start) | async-done | bytes 524320 | tf_op jit(solution)/shard_map/all_to_all | solution.py:9
  37.1 0.3 reduce_sum.34
  37.5 0.1 div.32
  37.6 0.1 copy.44
  37.7 0.6 select_reduce_fusion.2
  38.9 0.1 copy.45
  39.0 5.8 %custom-call.11 = f32[1,64,64]{2,1,0:T(8,128)S(1)} custom-call(f32[1,64,64]{2,1,0:T(8,128)S(1)} %fusion.13), custom_call_target="Cholesky" | custom-call | tf_op jit(solution)/shard_map/vmap(jit(cholesky))/cholesky | solution.py:54
  44.9 0.6 compare_reduce_fusion
  45.6 0.7 fusion.12
  46.2 4.9 %custom-call.12 = f32[1,1,64,64]{2,3,1,0:T(8,128)S(1)} custom-call(f32[1,1,64,64]{3,2,1,0:T(8,128)S(1)} %fusion.12), custom_call_target="InvertDiagBlocksLowerTriangular" | custom-call | tf_op jit(solution)/shard_map/vmap(jit(_cho_solve))/triangular_solve | solution.py:57
  51.1 0.3 fusion.16
  51.4 0.2 convolution_bitcast_fusion.2
  51.6 0.1 reshape.199
  51.7 0.1 copy.47
  51.8 0.1 reshape.207
  51.9 0.1 div.29
  51.9 0.1 copy.41
  52.0 0.6 select_reduce_fusion.3
  53.3 0.1 copy.42
  53.4 5.8 %custom-call.10 = f32[1,64,64]{2,1,0:T(8,128)S(1)} custom-call(f32[1,64,64]{2,1,0:T(8,128)S(1)} %fusion.14), custom_call_target="Cholesky" | custom-call | tf_op jit(solution)/shard_map/vmap(jit(cholesky))/cholesky | solution.py:53
  59.3 0.6 compare_reduce_fusion.1
  59.9 0.7 fusion.11
  60.6 4.9 %custom-call.13 = f32[1,1,64,64]{2,3,1,0:T(8,128)S(1)} custom-call(f32[1,1,64,64]{3,2,1,0:T(8,128)S(1)} %fusion.11), custom_call_target="InvertDiagBlocksLowerTriangular" | custom-call | tf_op jit(solution)/shard_map/vmap(jit(_cho_solve))/triangular_solve | solution.py:61
  65.5 0.3 fusion.19
  65.8 0.2 fusion.5
  65.9 0.1 copy.51
  66.0 0.1 convert_element_type.22
  66.1 0.2 broadcast_in_dim.21
  66.4 15.5 %all_to_all.26 = bf16[16,1,2,4096]{3,2,1,0:T(2,128)(2,1)S(1)} all-to-all(bf16[16,1,2,4096]{3,2,1,0:T(2,128)(2,1)S(1)} %broadcast_in_dim.21), channel_id=1, replica_groups=mesh['dp'=16,'layer'=16] {'dp'}, dimensions={0} | all-to-all | bytes 524288 | tf_op jit(solution)/shard_map/all_to_all | solution.py:9
  81.9 0.0 copy-done.1
  81.9 0.4 fusion.6
  82.3 0.1 reshape.215
  82.4 14.4 %all_to_all.27 = f32[16,1,128]{2,1,0:T(1,128)S(1)} all-to-all(f32[16,1,128]{2,1,0:T(1,128)S(1)} %reshape.215), channel_id=1, replica_groups=mesh['dp'=16,'layer'=16] {'dp'}, dimensions={0} | all-to-all | bytes 16384 | tf_op jit(solution)/shard_map/all_to_all | solution.py:81
  96.8 0.5 broadcast.79
  97.3 0.7 reduce.12
  97.9 0.1 reshape.216
  98.0 0.1 reshape.217
  98.1 9.5 %all_to_all.28 = f32[16,1,128]{2,1,0:T(1,128)S(1)} all-to-all(f32[16,1,128]{2,1,0:T(1,128)S(1)} %reshape.217), channel_id=1, replica_groups=mesh['dp'=16,'layer'=16] {'layer'}, dimensions={0} | all-to-all | bytes 16384 | tf_op jit(solution)/shard_map/all_to_all | solution.py:44
  107.6 0.7 reduce.13
  108.3 0.1 reshape.218
  108.4 0.6 broadcast_multiply_fusion
  (10 shorter events, 0.2 us)
Async XLA Ops:
  0.0 6.4 %copy-start = (bf16[1,2,128,4096]{3,2,1,0:T(8,128)(2,1)S(1)}, bf16[1,2,128,4096]{3,2,1,0:T(8,128)(2,1)}, u32[]{:S(2)}) copy-start(bf16[1,2,128,4096]{3,2,1,0:T(8,128)(2,1)} %param.8) | copy-start | bytes 6291460
  0.0 6.4 %copy-start.2 = (bf16[1,64,4096]{2,1,0:T(8,128)(2,1)S(1)}, bf16[1,64,4096]{2,1,0:T(8,128)(2,1)}, u32[]{:S(2)}) copy-start(bf16[1,64,4096]{2,1,0:T(8,128)(2,1)} %param.10) | copy-start | bytes 1572868
  8.6 73.2 %copy-start.1 = (bf16[1,64,4096]{2,1,0:T(8,128)(2,1)S(1)}, bf16[1,64,4096]{2,1,0:T(8,128)(2,1)}, u32[]{:S(2)}) copy-start(bf16[1,64,4096]{2,1,0:T(8,128)(2,1)} %param.12) | copy-start | bytes 1572868
  8.6 28.5 %all-to-all-start = ((f32[16,1,8192]{2,1,0:T(1,128)}), f32[16,1,8192]{2,1,0:T(1,128)S(1)}, u32[]{:S(2)}, u32[]{:S(2)}) async-start(f32[16,1,8192]{2,1,0:T(1,128)} %broadcast_in_dim.19), calls=%async_computation | async-start | bytes 1048576 | tf_op jit(solution)/shard_map/all_to_all | solution.py:9
where the time goes:
time: 111 us; the launch traced here: 109 us
  blocking collectives  39.4 us (35%)
  other arithmetic  27.7 us (25%)
  waiting for transfers between devices  16.8 us (15%)
  starting transfers between devices  11.3 us (10%)
  matrix products  8.67 us (8%)
  local copies, waits for them, and re-layouts  3.54 us (3%)
  between operations  1.51 us (1%)
    all_to_all x1, waiting for transfers between devices, sent_to_all(): lax.all_to_all(jnp.broadcast_to(value[None], (size, *value.shape)), axis,...  16.8 us
    all_to_all x1, blocking collectives, sent_to_all(): lax.all_to_all(jnp.broadcast_to(value[None], (size, *value.shape)), axis,...  15.5 us
    all_to_all x1, blocking collectives, local(): lax.all_to_all(local_scores, 'dp', split_axis=0, concat_axis=1, tiled=True)  14.4 us
    all_to_all x1, starting transfers between devices, sent_to_all(): lax.all_to_all(jnp.broadcast_to(value[None], (size, *value.shape)), axis,...  11.3 us
    all_to_all x1, blocking collectives, summed_on_arrival(): tiles = lax.all_to_all(cut_along(value, dim, size), axis, 0, 0, tiled=True)  9.46 us
    another operation x3, other arithmetic, precondition(): factor_out = jnp.linalg.cholesky(cov_out + damp_out * identity)  6.52 us
    another operation x3, other arithmetic, precondition(): factor_in = jnp.linalg.cholesky(cov_in + damp_in * identity)  6.52 us
    dot_general x1, matrix products, local(): jnp.einsum('lesd,lrd->lesr', grads, proj_out, preferred_element_type=jnp....  6.08 us
  transfers between devices with their start and end apart: 1, of which 1 were waited for; matrix products, arithmetic and copies ran while one was open for 0% of the time, Pallas kernels for 0%

commit v1 on v0

v1 whole, which is shorter than its diff:
```python
import functools

import jax
import jax.numpy as jnp
from jax import lax
from jax.experimental import pallas as pl
from jax.experimental.pallas import tpu as pltpu
from jax.sharding import PartitionSpec as P

MESH = pl.DeviceIdType.MESH
HIGHEST = lax.Precision.HIGHEST
CHUNK = 2048
PANEL = 4
NT = (((1,), (1,)), ((), ()))
TN = (((0,), (0,)), ((), ()))


def lanes(shape):
    return lax.broadcasted_iota(jnp.int32, shape, 1)


def rows_of(shape):
    return lax.broadcasted_iota(jnp.int32, shape, 0)


def inverses(a):
    size = a.shape[0]
    shape = a.shape
    left = lanes(shape) < size
    lane = lax.rem(lanes(shape), size)
    lane_row = lane[:1]
    row = rows_of(shape)

    def column(k):
        return jnp.where(
            left,
            jnp.broadcast_to(a[:, k : k + 1], shape),
            jnp.broadcast_to(a[:, size + k : size + k + 1], shape),
        )

    for first in range(0, size, PANEL):
        panel = [column(first + t) for t in range(PANEL)]
        for t in range(PANEL):
            k = first + t
            c = panel[t]
            p = 1.0 / c[k : k + 1]
            scaled = jnp.where(lane_row == k, p, a[k : k + 1] * p)
            is_row = row == k
            a = jnp.where(is_row, scaled, jnp.where(lane == k, 0.0, a) - c * scaled)
            for u in range(t + 1, PANEL):
                s = panel[u][k : k + 1] * p
                panel[u] = jnp.where(is_row, s, panel[u] - c * s)
    return a


def kernel(
    n,
    scale,
    acts,
    grads,
    proj_in,
    proj_out,
    queries,
    out,
    acts_v,
    grads_v,
    pin_v,
    pout_v,
    q_v,
    cov_v,
    cov_r,
    piece_v,
    f_v,
    own_g,
    g_v,
    c_v,
    s_v,
    s_r,
    load_sem,
    rs_send,
    rs_recv,
    ag_send,
    ag_recv,
    g_send,
    g_recv,
    s_send,
    s_recv,
):
    i = lax.axis_index("dp")
    l = lax.axis_index("layer")
    rank = 64
    part = rank // n
    act_chunks, grad_chunks = acts_v.shape[0], grads_v.shape[0]

    def chunk(ref, c):
        return ref.at[:, pl.ds(c * CHUNK, CHUNK)]

    loads = []

    def load(src, dst):
        copy = pltpu.make_async_copy(src, dst, load_sem.at[len(loads)])
        copy.start()
        loads.append(copy)
        return copy

    pin_load = load(proj_in, pin_v)
    act_loads = [load(chunk(acts, c), acts_v.at[c]) for c in range(act_chunks)]
    pout_load = load(proj_out, pout_v)
    grad_loads = [load(chunk(grads, c), grads_v.at[c]) for c in range(grad_chunks)]
    q_load = load(queries, q_v)

    barrier = pltpu.get_barrier_semaphore()

    def greet(d, _):
        pl.semaphore_signal(
            barrier, inc=1, device_id=(lax.rem(i + d, n), l), device_id_type=MESH
        )
        return 0

    def greet_far(j, _):
        pl.semaphore_signal(barrier, inc=1, device_id=(j, i), device_id_type=MESH)
        pl.semaphore_signal(barrier, inc=1, device_id=(l, j), device_id_type=MESH)
        return 0

    lax.fori_loop(1, n, greet, 0)
    lax.fori_loop(0, n, greet_far, 0)

    tokens = acts_v.shape[1]
    pin_load.wait()
    pa = jnp.zeros((tokens, rank), jnp.float32)
    for c in range(act_chunks):
        act_loads[c].wait()
        pa += lax.dot_general(
            acts_v[c],
            pin_v[:, c * CHUNK : (c + 1) * CHUNK],
            NT,
            preferred_element_type=jnp.float32,
        )
    pout_load.wait()
    pg = jnp.zeros((tokens, rank), jnp.float32)
    for c in range(grad_chunks):
        grad_loads[c].wait()
        pg += lax.dot_general(
            grads_v[c],
            pout_v[:, c * CHUNK : (c + 1) * CHUNK],
            NT,
            preferred_element_type=jnp.float32,
        )
    both = jnp.concatenate([pa, pg], axis=1)
    length = tokens // 2
    grams = [
        lax.dot_general(
            both[e * length : (e + 1) * length],
            both[e * length : (e + 1) * length],
            TN,
            precision=HIGHEST,
            preferred_element_type=jnp.float32,
        )
        for e in range(2)
    ]
    total = grams[0] + grams[1]
    left = lanes((rank, 2 * rank)) < rank
    cov = jnp.where(left, total[:rank], total[rank:])
    for p in range(n):
        cov_v[p] = cov[p * part : (p + 1) * part]
    grad = jnp.where(left, grams[0][rank:], pltpu.roll(grams[1][rank:], rank, 1))
    own_g[...] = grad

    pl.semaphore_wait(barrier, 3 * n - 1)

    def rs_copy(d):
        p = lax.rem(i + d, n)
        return pltpu.make_async_remote_copy(
            cov_v.at[p], cov_r.at[i], rs_send.at[p], rs_recv.at[i],
            device_id=(p, l), device_id_type=MESH,
        )

    def rs_from(d):
        p = lax.rem(i + d, n)
        return pltpu.make_async_remote_copy(
            cov_v.at[p], cov_r.at[p], rs_send.at[p], rs_recv.at[p],
            device_id=(p, l), device_id_type=MESH,
        )

    def ag_copy(d):
        p = lax.rem(i + d, n)
        return pltpu.make_async_remote_copy(
            piece_v, f_v.at[i], ag_send.at[p], ag_recv.at[i],
            device_id=(p, l), device_id_type=MESH,
        )

    def ag_from(d):
        p = lax.rem(i + d, n)
        return pltpu.make_async_remote_copy(
            piece_v, f_v.at[p], ag_send.at[p], ag_recv.at[p],
            device_id=(p, l), device_id_type=MESH,
        )

    def g_copy(d):
        p = lax.rem(i + d, n)
        return pltpu.make_async_remote_copy(
            own_g, g_v.at[i], g_send.at[p], g_recv.at[i],
            device_id=(p, l), device_id_type=MESH,
        )

    def g_from(d):
        p = lax.rem(i + d, n)
        return pltpu.make_async_remote_copy(
            own_g, g_v.at[p], g_send.at[p], g_recv.at[p],
            device_id=(p, l), device_id_type=MESH,
        )

    def each(action, lo=1, hi=n):
        def body(d, _):
            action(d)
            return 0

        lax.fori_loop(lo, hi, body, 0)

    early = 1 + (n - 1) // 3
    each(lambda d: rs_copy(d).start())
    each(lambda d: g_copy(d).start(), 1, early)
    cov_r[i] = cov_v[i]
    g_v[i] = own_g[...]
    each(lambda d: rs_from(d).wait_recv())
    piece = cov_r[0]
    for p in range(1, n):
        piece += cov_r[p]
    piece_v[...] = piece
    f_v[i] = piece
    each(lambda d: ag_copy(d).start())
    each(lambda d: g_copy(d).start(), early, n)
    each(lambda d: ag_from(d).wait_recv())

    f = jnp.concatenate([f_v[p] for p in range(n)], axis=0) / jnp.float32(tokens * n)
    on_diagonal = lax.rem(lanes(f.shape), rank) == rows_of(f.shape)
    diagonal = jnp.sum(jnp.where(on_diagonal, f, 0.0), axis=0, keepdims=True)
    in_left = lanes(diagonal.shape) < rank
    trace_in = jnp.sum(jnp.where(in_left, diagonal, 0.0), axis=1, keepdims=True)
    trace_out = jnp.sum(jnp.where(in_left, 0.0, diagonal), axis=1, keepdims=True)
    damp = jnp.where(in_left, 0.1 * trace_in / rank, 0.1 * trace_out / rank)
    f = jnp.where(on_diagonal, f + damp, f)
    inv = inverses(f)
    turned = pltpu.roll(inv, rank, 1)
    twice_in = jnp.concatenate(
        [jnp.where(left, inv, 0.0), jnp.where(left, 0.0, turned)], axis=0
    )
    inv_out = turned[:, :rank]

    each(lambda d: g_from(d).wait_recv())
    for p in range(n):
        half = lax.dot_general(
            g_v[p], twice_in, (((1,), (0,)), ((), ())),
            precision=HIGHEST, preferred_element_type=jnp.float32,
        )
        c_v[p * rank : (p + 1) * rank] = lax.dot_general(
            inv_out, half, (((1,), (0,)), ((), ())),
            precision=HIGHEST, preferred_element_type=jnp.float32,
        )

    q_load.wait()
    in_left = lanes((n, 2 * rank)) < rank
    scores = jnp.zeros((2 * n, q_v.shape[0]), jnp.float32)
    for o in range(0, rank, 4):
        firsts, seconds = [], []
        for o2 in (o, o + 2):
            a = c_v[pl.ds(o2, n, stride=rank), :]
            b = c_v[pl.ds(o2 + 1, n, stride=rank), :]
            firsts.append(jnp.where(in_left, a, pltpu.roll(b, rank, 1)))
            seconds.append(jnp.where(in_left, pltpu.roll(a, rank, 1), b))
        flat = jnp.concatenate(
            [jnp.concatenate(firsts, axis=1), jnp.concatenate(seconds, axis=1)], axis=0
        ).astype(jnp.bfloat16)
        scores += lax.dot_general(
            flat, q_v[:, o * rank : (o + 4) * rank], NT, preferred_element_type=jnp.float32
        )
    pairs = jnp.concatenate([scores[:n], scores[n:]], axis=1)
    for p in range(n):
        s_v[p] = pairs[p : p + 1]

    def s_copy(p):
        return pltpu.make_async_remote_copy(
            s_v.at[p], s_r.at[l], s_send.at[p], s_recv.at[l],
            device_id=(p, i), device_id_type=MESH,
        )

    def s_from(k):
        return pltpu.make_async_remote_copy(
            s_v.at[k], s_r.at[k], s_send.at[k], s_recv.at[k],
            device_id=(l, k), device_id_type=MESH,
        )

    def unless_self(other, action):
        @pl.when(jnp.logical_or(i != l, other != i))
        def _():
            action(other)

    each(lambda p: unless_self(p, lambda q: s_copy(q).start()), 0, n)

    @pl.when(i == l)
    def _():
        s_r[l] = s_v[i]

    each(lambda k: unless_self(k, lambda q: s_from(q).wait_recv()), 0, n)
    result = s_r[0]
    for k in range(1, n):
        result += s_r[k]
    result = result / scale
    out[0:1, :] = result[:, :rank]
    out[1:2, :] = pltpu.roll(result, rank, 1)[:, :rank]

    each(lambda d: rs_copy(d).wait_send())
    each(lambda d: ag_copy(d).wait_send())
    each(lambda d: g_copy(d).wait_send())
    each(lambda p: unless_self(p, lambda q: s_copy(q).wait_send()), 0, n)


def local(acts, grads, proj_in, proj_out, query_grads):
    n = lax.axis_size("dp")
    layer_count, examples, length, width = acts.shape
    hidden = grads.shape[3]
    rank = proj_in.shape[1]
    queries, flat = query_grads.shape[1:]
    tokens = examples * length
    part = rank // n
    scale = float(flat * lax.axis_size("layer") * layer_count * length) ** 0.5
    f32, bf16 = jnp.float32, jnp.bfloat16
    dma = pltpu.SemaphoreType.DMA
    act_chunks, grad_chunks = width // CHUNK, hidden // CHUNK
    hbm = pl.BlockSpec(memory_space=pl.ANY)
    return pl.pallas_call(
        functools.partial(kernel, n, scale),
        out_shape=jax.ShapeDtypeStruct((examples, queries), f32),
        in_specs=[hbm] * 5,
        out_specs=pl.BlockSpec(memory_space=pltpu.VMEM),
        scratch_shapes=[
            pltpu.VMEM((act_chunks, tokens, CHUNK), bf16),
            pltpu.VMEM((grad_chunks, tokens, CHUNK), bf16),
            pltpu.VMEM((rank, width), bf16),
            pltpu.VMEM((rank, hidden), bf16),
            pltpu.VMEM((queries, flat), bf16),
            pltpu.VMEM((n, part, 2 * rank), f32),
            pltpu.VMEM((n, part, 2 * rank), f32),
            pltpu.VMEM((part, 2 * rank), f32),
            pltpu.VMEM((n, part, 2 * rank), f32),
            pltpu.VMEM((rank, 2 * rank), f32),
            pltpu.VMEM((n, rank, 2 * rank), f32),
            pltpu.VMEM((n * rank, 2 * rank), f32),
            pltpu.VMEM((n, 1, 2 * rank), f32),
            pltpu.VMEM((n, 1, 2 * rank), f32),
            dma((act_chunks + grad_chunks + 3,)),
        ]
        + [dma((n,))] * 8,
        compiler_params=pltpu.CompilerParams(
            collective_id=0, has_side_effects=True, vmem_limit_bytes=60 * 1024 * 1024
        ),
    )(
        acts.reshape(tokens, width),
        grads.reshape(tokens, hidden),
        proj_in[0],
        proj_out[0],
        query_grads[0],
    )


def solution(mesh):
    return jax.shard_map(
        local,
        mesh=mesh,
        in_specs=(
            P("layer", "dp", None, None),
            P("layer", "dp", None, None),
            P("layer", None, None),
            P("layer", None, None),
            P("layer", "dp", None),
        ),
        out_specs=P("dp", "layer"),
        check_vma=False,
    )
```

time: 111 us -> 44.3 us (0.40); the launches traced: 109 us -> 43.5 us
  Pallas kernels: 0 us -> 42.3 us
  blocking collectives: 39.4 us -> 0 us
  other arithmetic: 27.7 us -> 0 us
  waiting for transfers between devices: 16.8 us -> 0 us
  starting transfers between devices: 11.3 us -> 0 us
  matrix products: 8.67 us -> 0 us
  local copies, waits for them, and re-layouts: 3.54 us -> 1.24 us
  between operations: 1.51 us -> 0.01 us
    pallas_call x0 -> x1, Pallas kernels: none -> 42.3 us  [local(): pl.pallas_call(functools.partial(kernel, n, scale), out_shape=jax.ShapeDt...]
    all_to_all x3 -> x0, blocking collectives: 39.4 us -> none  [the longest x1 15.5 us: sent_to_all(): lax.all_to_all(jnp.broadcast_to(value[None], (size, *value.shape)), axis,...]
    another operation x10 -> x0, other arithmetic: 24.1 us -> none  [the longest x3 6.52 us: precondition(): factor_out = jnp.linalg.cholesky(cov_out + damp_out * identity)]
    all_to_all x1 -> x0, waiting for transfers between devices: 16.8 us -> none  [sent_to_all(): lax.all_to_all(jnp.broadcast_to(value[None], (size, *value.shape)), axis,...]
    all_to_all x1 -> x0, starting transfers between devices: 11.3 us -> none  [sent_to_all(): lax.all_to_all(jnp.broadcast_to(value[None], (size, *value.shape)), axis,...]
    dot_general x6 -> x0, matrix products: 7.85 us -> none  [the longest x1 6.08 us: local(): jnp.einsum('lesd,lrd->lesr', grads, proj_out, preferred_element_type=jnp....]
    reduce_sum x4 -> x0, other arithmetic: 1.62 us -> none  [the longest x1 0.63 us: precondition(): damp_in = 0.1 * jnp.trace(cov_in) / size]
    broadcast_in_dim x2 -> x0, local copies, waits for them, and re-layouts: 1.4 us -> none  [sent_to_all(): jnp.broadcast_to(value[None], (size, *value.shape))]
  transfers between devices with their start and end apart: 1 -> 0, of which waited for: 1 -> 0; matrix products, arithmetic and copies ran while one was open for 0% -> 0% of each run, Pallas kernels for 0% -> 0%
where the time goes in v1:
time: 44.3 us; the launch traced here: 43.5 us
  Pallas kernels  42.3 us (95%)
  local copies, waits for them, and re-layouts  1.24 us (3%)
    pallas_call x1, Pallas kernels, local(): pl.pallas_call(functools.partial(kernel, n, scale), out_shape=jax.ShapeDt...  42.3 us
    unnamed x1, local copies, waits for them, and re-layouts  1.24 us

profile of v1, /device:TPU:2, one launch (start us, length us, event | category | flops | bytes accessed | tf_op | source)
XLA Modules:
  0.0 43.5 jit_solution(14191720330356703923)
XLA Ops:
  0.0 42.3 %shard_map.55 = f32[2,64]{1,0:T(2,128)} custom-call(bf16[256,4096]{1,0:T(8,128)(2,1)} %bitcast.6, bf16[256,14336]{1,0:T(8,128)(2,1)} %bitcast.5, bf16[64,4096]{1,0:T(8,128)(2,1)} %bitcast.8, bf16[64,14336]{1,0:T(8,128)(2,1)} %bitcast.7, bf16[64,4096]{1,0:T(8,128)(2,1)} %bitcast.9), custom_call_target="tpu_custom_call" | custom-call | tf_op jit(solution)/shard_map/pallas_call | solution.py:331
  42.3 1.2 %copy.7 = f32[2,64]{1,0:T(2,128)} copy(f32[2,64]{1,0:T(2,128)} %shard_map.55) | data formatting | bytes 1024

commit v2 on v1

v2 whole, which is shorter than its diff:
```python
import functools

import jax
import jax.numpy as jnp
from jax import lax
from jax.experimental import pallas as pl
from jax.experimental.pallas import tpu as pltpu
from jax.sharding import PartitionSpec as P

MESH = pl.DeviceIdType.MESH
HIGHEST = lax.Precision.HIGHEST
CHUNK = 2048
PANEL = 8
EARLY = 5
NT = (((1,), (1,)), ((), ()))
TN = (((0,), (0,)), ((), ()))


def lanes(shape):
    return lax.broadcasted_iota(jnp.int32, shape, 1)


def rows_of(shape):
    return lax.broadcasted_iota(jnp.int32, shape, 0)


def inverses(a):
    size = a.shape[0]
    shape = a.shape
    left = lanes(shape) < size
    lane = lax.rem(lanes(shape), size)
    lane_row = lane[:1]
    row = rows_of(shape)

    def column(k):
        return jnp.where(
            left,
            jnp.broadcast_to(a[:, k : k + 1], shape),
            jnp.broadcast_to(a[:, size + k : size + k + 1], shape),
        )

    for first in range(0, size, PANEL):
        panel = [column(first + t) for t in range(PANEL)]
        for t in range(PANEL):
            k = first + t
            c = panel[t]
            p = 1.0 / c[k : k + 1]
            scaled = jnp.where(lane_row == k, p, a[k : k + 1] * p)
            is_row = row == k
            a = jnp.where(is_row, scaled, jnp.where(lane == k, 0.0, a) - c * scaled)
            for u in range(t + 1, PANEL):
                s = panel[u][k : k + 1] * p
                panel[u] = jnp.where(is_row, s, panel[u] - c * s)
    return a


def split3(x):
    high = x.astype(jnp.bfloat16)
    rest = x - high.astype(jnp.float32)
    mid = rest.astype(jnp.bfloat16)
    low = (rest - mid.astype(jnp.float32)).astype(jnp.bfloat16)
    return high, mid, low


def moving(x):
    high, mid, low = split3(x)
    return jnp.concatenate([high, mid], axis=1), jnp.concatenate([high, low], axis=1)


def standing(w):
    high, mid, low = split3(w)
    row = jnp.concatenate([high, mid], axis=1)
    return jnp.concatenate([row, row], axis=0), jnp.concatenate([low, high], axis=0)


def product(pair, weights):
    width = weights[1].shape[1]
    wide = jnp.dot(pair[0], weights[0], preferred_element_type=jnp.float32)
    rest = jnp.dot(pair[1], weights[1], preferred_element_type=jnp.float32)
    return wide[:, :width] + (wide[:, width:] + rest)


def kernel(
    n,
    acts,
    grads,
    proj_in,
    proj_out,
    queries,
    out,
    acts_v,
    grads_v,
    pin_v,
    pout_v,
    q_v,
    cov_v,
    cov_r,
    piece_v,
    f_v,
    own_g,
    g_v,
    c_v,
    s_v,
    s_r,
    load_sem,
    send_sem,
    recv_sem,
):
    i = lax.axis_index("dp")
    l = lax.axis_index("layer")
    rank = 64
    part = rank // n
    ring = n // 2
    act_chunks, grad_chunks = acts_v.shape[0], grads_v.shape[0]
    column, place = i // ring, lax.rem(i, ring)

    far_first = sorted(range(1, ring), key=lambda z: -min(z, ring - z))
    offsets = [(1, z) for z in far_first] + [(0, z) for z in far_first] + [(1, 0)]
    offsets.sort(key=lambda o: -(2 * o[0] + min(o[1], ring - o[1])))
    peers = [
        lax.rem(column + dh, 2) * ring + lax.rem(place + dz, ring) for dh, dz in offsets
    ]

    loads = []

    def load(src, dst):
        copy = pltpu.make_async_copy(src, dst, load_sem.at[len(loads)])
        copy.start()
        loads.append(copy)
        return copy

    def chunk(ref, c):
        return ref.at[:, pl.ds(c * CHUNK, CHUNK)]

    pin_load = load(proj_in, pin_v)
    act_loads = [load(chunk(acts, c), acts_v.at[c]) for c in range(act_chunks)]
    pout_load = load(proj_out, pout_v)
    grad_loads = [load(chunk(grads, c), grads_v.at[c]) for c in range(grad_chunks)]
    q_load = load(queries, q_v)

    barrier = pltpu.get_barrier_semaphore()

    def greet(dp, layer):
        pl.semaphore_signal(barrier, inc=1, device_id=(dp, layer), device_id_type=MESH)

    def greet_far(j, _):
        greet(j, i)
        greet(l, j)
        return 0

    lax.fori_loop(0, n, greet_far, 0)
    for p in peers:
        greet(p, l)
    tokens = acts_v.shape[1]
    length = tokens // 2

    def project(x_v, w_v, first_load, x_loads):
        sums = [jnp.zeros((length, rank), jnp.float32)] * 2
        first_load.wait()
        for c, arrival in enumerate(x_loads):
            arrival.wait()
            for e in range(2):
                sums[e] += lax.dot_general(
                    x_v[c, e * length : (e + 1) * length],
                    w_v[:, c * CHUNK : (c + 1) * CHUNK],
                    NT,
                    preferred_element_type=jnp.float32,
                )
        return sums

    pa = project(acts_v, pin_v, pin_load, act_loads)
    pg = project(grads_v, pout_v, pout_load, grad_loads)
    grams = []
    for e in range(2):
        both = jnp.concatenate([pa[e], pg[e]], axis=1)
        grams.append(
            lax.dot_general(
                both, both, TN, precision=HIGHEST, preferred_element_type=jnp.float32
            )
        )
    total = grams[0] + grams[1]
    left = lanes((rank, 2 * rank)) < rank
    cov = jnp.where(left, total[:rank], total[rank:])
    for p in range(n):
        cov_v[p] = cov[p * part : (p + 1) * part]
    own_g[...] = jnp.where(left, pltpu.roll(grams[0][:rank], rank, 1), grams[1][:rank])
    pl.semaphore_wait(barrier, 3 * n - 1)

    def push(src, dst, phase, device):
        return pltpu.make_async_remote_copy(
            src, dst, send_sem.at[phase], recv_sem.at[phase],
            device_id=device, device_id_type=MESH,
        )

    def all_of(slots, sem):
        view = slots.at[pl.ds(0, n - 1)]
        pltpu.make_async_copy(view, view, sem).wait()

    for p in peers:
        push(cov_v.at[p], cov_r.at[i], 0, (p, l)).start()
    for p in peers[:EARLY]:
        push(own_g, g_v.at[i], 2, (p, l)).start()
    cov_r[i] = cov_v[i]
    g_v[i] = own_g[...]
    all_of(cov_r, recv_sem.at[0])
    piece = cov_r[0]
    for p in range(1, n):
        piece += cov_r[p]
    piece_v[...] = piece
    f_v[i] = piece
    for p in peers:
        push(piece_v, f_v.at[i], 1, (p, l)).start()
    for p in peers[EARLY:]:
        push(own_g, g_v.at[i], 2, (p, l)).start()
    all_of(f_v, recv_sem.at[1])
    f = jnp.concatenate([f_v[p] for p in range(n)], axis=0) / jnp.float32(tokens * n)
    on_diagonal = lax.rem(lanes(f.shape), rank) == rows_of(f.shape)
    diagonal = jnp.sum(jnp.where(on_diagonal, f, 0.0), axis=0, keepdims=True)
    in_left = lanes(diagonal.shape) < rank
    trace_in = jnp.sum(jnp.where(in_left, diagonal, 0.0), axis=1, keepdims=True)
    trace_out = jnp.sum(jnp.where(in_left, 0.0, diagonal), axis=1, keepdims=True)
    damp = jnp.where(in_left, 0.1 * trace_in / rank, 0.1 * trace_out / rank)
    f = jnp.where(on_diagonal, f + damp, f)
    inv = inverses(f)
    turned = pltpu.roll(inv, rank, 1)
    twice_in = standing(
        jnp.concatenate([jnp.where(left, inv, 0.0), jnp.where(left, 0.0, turned)], axis=0)
    )
    twice_out = standing(
        jnp.concatenate([jnp.where(left, turned, 0.0), jnp.where(left, 0.0, inv)], axis=0)
    )
    all_of(g_v, recv_sem.at[2])
    block = 2 * rank
    for b in range(n // 2):
        pair = moving(jnp.concatenate([g_v[2 * b], g_v[2 * b + 1]], axis=0))
        half = product(pair, twice_out)
        c_v[b * block : (b + 1) * block] = product(moving(half.T), twice_in)
    q_load.wait()
    in_left = lanes((n, 2 * rank)) < rank
    scores = jnp.zeros((2 * n, q_v.shape[0]), jnp.float32)
    for o in range(0, rank, 4):
        firsts, seconds = [], []
        for o2 in (o, o + 2):
            a = c_v[pl.ds(o2, n, stride=rank), :]
            b = c_v[pl.ds(o2 + 1, n, stride=rank), :]
            firsts.append(jnp.where(in_left, a, pltpu.roll(b, rank, 1)))
            seconds.append(jnp.where(in_left, pltpu.roll(a, rank, 1), b))
        flat = jnp.concatenate(
            [jnp.concatenate(firsts, axis=1), jnp.concatenate(seconds, axis=1)], axis=0
        ).astype(jnp.bfloat16)
        scores += lax.dot_general(
            flat, q_v[:, o * rank : (o + 4) * rank], NT, preferred_element_type=jnp.float32
        )
    for p in range(n):
        at = (p % 2) * n + p // 2 * 2
        s_v[p] = scores[at : at + 2]
    def unless_self(other, action):
        @pl.when(jnp.logical_or(i != l, other != i))
        def _():
            action(other)

    def s_copy(p):
        return pltpu.make_async_remote_copy(
            s_v.at[p], s_r.at[l], send_sem.at[3], recv_sem.at[3],
            device_id=(p, i), device_id_type=MESH,
        )

    for p in range(n):
        unless_self(p, lambda q: s_copy(q).start())

    @pl.when(i == l)
    def _():
        s_r[l] = s_v[i]

    for phase, slots in enumerate((cov_r, f_v, g_v)):
        all_of(slots, send_sem.at[phase])

    def last(sem):
        @pl.when(i == l)
        def _():
            all_of(s_r, sem)

        @pl.when(i != l)
        def _():
            pltpu.make_async_copy(s_r, s_r, sem).wait()

    last(recv_sem.at[3])
    result = s_r[0]
    for k in range(1, n):
        result += s_r[k]
    out[...] = result
    last(send_sem.at[3])


def local(acts, grads, proj_in, proj_out, query_grads):
    n = lax.axis_size("dp")
    layer_count, examples, length, width = acts.shape
    hidden = grads.shape[3]
    rank = proj_in.shape[1]
    queries, flat = query_grads.shape[1:]
    tokens = examples * length
    part = rank // n
    f32, bf16 = jnp.float32, jnp.bfloat16
    dma = pltpu.SemaphoreType.DMA
    act_chunks, grad_chunks = width // CHUNK, hidden // CHUNK
    hbm = pl.BlockSpec(memory_space=pl.ANY)
    total = pl.pallas_call(
        functools.partial(kernel, n),
        out_shape=jax.ShapeDtypeStruct((examples, queries), f32),
        in_specs=[hbm] * 5,
        out_specs=pl.BlockSpec(memory_space=pltpu.VMEM),
        scratch_shapes=[
            pltpu.VMEM((act_chunks, tokens, CHUNK), bf16),
            pltpu.VMEM((grad_chunks, tokens, CHUNK), bf16),
            pltpu.VMEM((rank, width), bf16),
            pltpu.VMEM((rank, hidden), bf16),
            pltpu.VMEM((queries, flat), bf16),
            pltpu.VMEM((n, part, 2 * rank), f32),
            pltpu.VMEM((n, part, 2 * rank), f32),
            pltpu.VMEM((part, 2 * rank), f32),
            pltpu.VMEM((n, part, 2 * rank), f32),
            pltpu.VMEM((rank, 2 * rank), f32),
            pltpu.VMEM((n, rank, 2 * rank), f32),
            pltpu.VMEM((n * rank, 2 * rank), f32),
            pltpu.VMEM((n, examples, queries), f32),
            pltpu.VMEM((n, examples, queries), f32),
            dma((act_chunks + grad_chunks + 3,)),
            dma((4,)),
            dma((4,)),
        ],
        compiler_params=pltpu.CompilerParams(
            collective_id=0, has_side_effects=True, vmem_limit_bytes=60 * 1024 * 1024
        ),
    )(
        acts.reshape(tokens, width),
        grads.reshape(tokens, hidden),
        proj_in[0],
        proj_out[0],
        query_grads[0],
    )
    layers_all = layer_count * lax.axis_size("layer")
    return total / jnp.sqrt(jnp.float32(flat * layers_all * length))


def solution(mesh):
    return jax.shard_map(
        local,
        mesh=mesh,
        in_specs=(
            P("layer", "dp", None, None),
            P("layer", "dp", None, None),
            P("layer", None, None),
            P("layer", None, None),
            P("layer", "dp", None),
        ),
        out_specs=P("dp", "layer"),
        check_vma=False,
    )
```

time: 44.3 us -> 37.6 us (0.85)
  Pallas kernels: 42.3 us -> 35.7 us
  other arithmetic: 0 us -> 1.24 us
  local copies, waits for them, and re-layouts: 1.24 us -> 0 us
    pallas_call x1, Pallas kernels: 42.3 us -> 35.7 us  [local(): pl.pallas_call(functools.partial(kernel, n), out_shape=jax.ShapeDtypeStru...]
    div x0 -> x1, other arithmetic: none -> 1.24 us  [local(): return total / jnp.sqrt(jnp.float32(flat * layers_all * length))]
    unnamed x1 -> x0, local copies, waits for them, and re-layouts: 1.24 us -> none
where the time goes in v2:
time: 37.6 us; the launch traced here: 36.9 us
  Pallas kernels  35.7 us (95%)
  other arithmetic  1.24 us (3%)
    pallas_call x1, Pallas kernels, local(): pl.pallas_call(functools.partial(kernel, n), out_shape=jax.ShapeDtypeStru...  35.7 us
    div x1, other arithmetic, local(): return total / jnp.sqrt(jnp.float32(flat * layers_all * length))  1.24 us

profile of v2, /device:TPU:2, one launch (start us, length us, event | category | flops | bytes accessed | tf_op | source)
XLA Modules:
  0.0 36.9 jit_solution(13159243788544918314)
XLA Ops:
  0.0 35.7 %shard_map.55 = f32[2,64]{1,0:T(2,128)} custom-call(bf16[256,4096]{1,0:T(8,128)(2,1)} %bitcast.6, bf16[256,14336]{1,0:T(8,128)(2,1)} %bitcast.5, bf16[64,4096]{1,0:T(8,128)(2,1)} %bitcast.8, bf16[64,14336]{1,0:T(8,128)(2,1)} %bitcast.7, bf16[64,4096]{1,0:T(8,128)(2,1)} %bitcast.9), custom_call_target="tpu_custom_call" | custom-call | tf_op jit(solution)/shard_map/pallas_call | solution.py:307
  35.7 1.2 %broadcast_multiply_fusion = f32[2,64]{1,0:T(2,128)} fusion(f32[2,64]{1,0:T(2,128)} %shard_map.55), kind=kLoop, calls=%fused_computation | loop fusion | flops 128 | bytes 1024 | tf_op jit(solution)/shard_map/div | solution.py:342

commit v3 on v2

--- a/solution.py
+++ b/solution.py
@@ -28,9 +28,8 @@
     size = a.shape[0]
     shape = a.shape
     left = lanes(shape) < size
-    lane = lax.rem(lanes(shape), size)
-    lane_row = lane[:1]
-    row = rows_of(shape)
+    lane_row = lax.rem(lanes((1, shape[1])), size)
+    row8 = rows_of((8, shape[1]))
 
     def column(k):
         return jnp.where(
@@ -39,18 +38,35 @@
             jnp.broadcast_to(a[:, size + k : size + k + 1], shape),
         )
 
+    def with_rows(x, k, first, second):
+        at = k // 8 * 8
+        group = x[at : at + 8]
+        group = jnp.where(row8 == k - at, first, jnp.where(row8 == k + 1 - at, second, group))
+        pieces = [x[:at]] * (at > 0) + [group] + [x[at + 8 :]] * (at + 8 < size)
+        return jnp.concatenate(pieces, axis=0)
+
     for first in range(0, size, PANEL):
         panel = [column(first + t) for t in range(PANEL)]
-        for t in range(PANEL):
+        for t in range(0, PANEL, 2):
             k = first + t
-            c = panel[t]
-            p = 1.0 / c[k : k + 1]
-            scaled = jnp.where(lane_row == k, p, a[k : k + 1] * p)
-            is_row = row == k
-            a = jnp.where(is_row, scaled, jnp.where(lane == k, 0.0, a) - c * scaled)
-            for u in range(t + 1, PANEL):
-                s = panel[u][k : k + 1] * p
-                panel[u] = jnp.where(is_row, s, panel[u] - c * s)
+            c1, c2 = panel[t], panel[t + 1]
+            a11, a12, a22 = c1[k : k + 1], c1[k + 1 : k + 2], c2[k + 1 : k + 2]
+            by_det = 1.0 / (a11 * a22 - a12 * a12)
+            b11, b12, b22 = a22 * by_det, -a12 * by_det, a11 * by_det
+
+            def solved(x1, x2):
+                return b11 * x1 + b12 * x2, b12 * x1 + b22 * x2
+
+            is_first, is_second = lane_row == k, lane_row == k + 1
+            s1, s2 = solved(a[k : k + 1], a[k + 1 : k + 2])
+            s1 = jnp.where(is_first, b11, jnp.where(is_second, b12, s1))
+            s2 = jnp.where(is_first, b12, jnp.where(is_second, b22, s2))
+            rest = jnp.where(jnp.logical_or(is_first, is_second), 0.0, a)
+            a = with_rows(rest - (c1 * s1 + c2 * s2), k, s1, s2)
+            for u in range(t + 2, PANEL):
+                x = panel[u]
+                u1, u2 = solved(x[k : k + 1], x[k + 1 : k + 2])
+                panel[u] = with_rows(x - (c1 * u1 + c2 * u2), k, u1, u2)
     return a
 
 
@@ -105,21 +121,25 @@
     load_sem,
     send_sem,
     recv_sem,
+    g_sem,
 ):
     i = lax.axis_index("dp")
     l = lax.axis_index("layer")
     rank = 64
-    part = rank // n
     ring = n // 2
+    part = rank // ring
     act_chunks, grad_chunks = acts_v.shape[0], grads_v.shape[0]
     column, place = i // ring, lax.rem(i, ring)
 
     far_first = sorted(range(1, ring), key=lambda z: -min(z, ring - z))
     offsets = [(1, z) for z in far_first] + [(0, z) for z in far_first] + [(1, 0)]
     offsets.sort(key=lambda o: -(2 * o[0] + min(o[1], ring - o[1])))
-    peers = [
-        lax.rem(column + dh, 2) * ring + lax.rem(place + dz, ring) for dh, dz in offsets
-    ]
+
+    def member(dh, dz):
+        return lax.rem(column + dh, 2) * ring + lax.rem(place + dz, ring)
+
+    peers = [member(*offset) for offset in offsets]
+    partner = member(1, 0)
 
     loads = []
 
@@ -181,39 +201,54 @@
     total = grams[0] + grams[1]
     left = lanes((rank, 2 * rank)) < rank
     cov = jnp.where(left, total[:rank], total[rank:])
-    for p in range(n):
-        cov_v[p] = cov[p * part : (p + 1) * part]
+    for z in range(ring):
+        cov_v[z] = cov[z * part : (z + 1) * part]
     own_g[...] = jnp.where(left, pltpu.roll(grams[0][:rank], rank, 1), grams[1][:rank])
     pl.semaphore_wait(barrier, 3 * n - 1)
 
-    def push(src, dst, phase, device):
+    def push(src, dst, send, recv, dp):
         return pltpu.make_async_remote_copy(
-            src, dst, send_sem.at[phase], recv_sem.at[phase],
-            device_id=device, device_id_type=MESH,
-        )
-
-    def all_of(slots, sem):
-        view = slots.at[pl.ds(0, n - 1)]
+            src, dst, send, recv, device_id=(dp, l), device_id_type=MESH
+        )
+
+    def all_of(slots, count, sem):
+        view = slots.at[pl.ds(0, count)]
         pltpu.make_async_copy(view, view, sem).wait()
 
-    for p in peers:
-        push(cov_v.at[p], cov_r.at[i], 0, (p, l)).start()
-    for p in peers[:EARLY]:
-        push(own_g, g_v.at[i], 2, (p, l)).start()
-    cov_r[i] = cov_v[i]
+    def share(dz):
+        push(own_g, g_v.at[i], send_sem.at[2], g_sem.at[place], member(0, dz)).start()
+
+    def forward(dz):
+        z = lax.rem(place + ring - dz, ring)
+        block = g_v.at[column * ring + z]
+        push(own_g, block, send_sem.at[2], g_sem.at[z], i).wait_recv()
+        push(block, block, send_sem.at[2], recv_sem.at[2], partner).start()
+
+    for dz in far_first:
+        push(
+            cov_v.at[lax.rem(place + dz, ring)], cov_r.at[place],
+            send_sem.at[0], recv_sem.at[0], member(0, dz),
+        ).start()
+    push(own_g, g_v.at[i], send_sem.at[2], recv_sem.at[2], partner).start()
+    for dz in far_first[:EARLY]:
+        share(dz)
+    cov_r[place] = cov_v[place]
     g_v[i] = own_g[...]
-    all_of(cov_r, recv_sem.at[0])
+    all_of(cov_r, ring - 1, recv_sem.at[0])
     piece = cov_r[0]
-    for p in range(1, n):
-        piece += cov_r[p]
+    for z in range(1, ring):
+        piece += cov_r[z]
     piece_v[...] = piece
     f_v[i] = piece
     for p in peers:
-        push(piece_v, f_v.at[i], 1, (p, l)).start()
-    for p in peers[EARLY:]:
-        push(own_g, g_v.at[i], 2, (p, l)).start()
-    all_of(f_v, recv_sem.at[1])
-    f = jnp.concatenate([f_v[p] for p in range(n)], axis=0) / jnp.float32(tokens * n)
+        push(piece_v, f_v.at[i], send_sem.at[1], recv_sem.at[1], p).start()
+    for dz in far_first[EARLY:]:
+        share(dz)
+    for dz in far_first:
+        forward(dz)
+    all_of(f_v, n - 1, recv_sem.at[1])
+    f = jnp.concatenate([f_v[z] + f_v[ring + z] for z in range(ring)], axis=0)
+    f = f / jnp.float32(tokens * n)
     on_diagonal = lax.rem(lanes(f.shape), rank) == rows_of(f.shape)
     diagonal = jnp.sum(jnp.where(on_diagonal, f, 0.0), axis=0, keepdims=True)
     in_left = lanes(diagonal.shape) < rank
@@ -229,12 +264,20 @@
     twice_out = standing(
         jnp.concatenate([jnp.where(left, turned, 0.0), jnp.where(left, 0.0, inv)], axis=0)
     )
-    all_of(g_v, recv_sem.at[2])
+    all_of(g_v, ring, recv_sem.at[2])
     block = 2 * rank
-    for b in range(n // 2):
-        pair = moving(jnp.concatenate([g_v[2 * b], g_v[2 * b + 1]], axis=0))
-        half = product(pair, twice_out)
-        c_v[b * block : (b + 1) * block] = product(moving(half.T), twice_in)
+    count = n // 2
+    g_rows = [
+        g_v[h * count : (h + 1) * count].reshape(count * rank, block) for h in range(2)
+    ]
+    halves = [product(moving(rows), twice_out) for rows in g_rows]
+    for h in range(2):
+        turned_rows = jnp.concatenate(
+            [halves[h][b * block : (b + 1) * block].T for b in range(count // 2)], axis=0
+        )
+        halves[h] = moving(turned_rows)
+    for h in range(2):
+        c_v[h * count * rank : (h + 1) * count * rank] = product(halves[h], twice_in)
     q_load.wait()
     in_left = lanes((n, 2 * rank)) < rank
     scores = jnp.zeros((2 * n, q_v.shape[0]), jnp.float32)
@@ -272,17 +315,18 @@
     def _():
         s_r[l] = s_v[i]
 
-    for phase, slots in enumerate((cov_r, f_v, g_v)):
-        all_of(slots, send_sem.at[phase])
+    all_of(cov_r, ring - 1, send_sem.at[0])
+    all_of(f_v, n - 1, send_sem.at[1])
+    all_of(g_v, n - 1, send_sem.at[2])
 
     def last(sem):
         @pl.when(i == l)
         def _():
-            all_of(s_r, sem)
+            all_of(s_r, n - 1, sem)
 
         @pl.when(i != l)
         def _():
-            pltpu.make_async_copy(s_r, s_r, sem).wait()
+            all_of(s_r, n, sem)
 
     last(recv_sem.at[3])
     result = s_r[0]
@@ -299,14 +343,15 @@
     rank = proj_in.shape[1]
     queries, flat = query_grads.shape[1:]
     tokens = examples * length
-    part = rank // n
+    ring = n // 2
+    part = rank // ring
     f32, bf16 = jnp.float32, jnp.bfloat16
     dma = pltpu.SemaphoreType.DMA
     act_chunks, grad_chunks = width // CHUNK, hidden // CHUNK
     hbm = pl.BlockSpec(memory_space=pl.ANY)
     total = pl.pallas_call(
         functools.partial(kernel, n),
-        out_shape=jax.ShapeDtypeStruct((examples, queries), f32),
+        out_shape=pltpu.VMEM((examples, queries), f32),
         in_specs=[hbm] * 5,
         out_specs=pl.BlockSpec(memory_space=pltpu.VMEM),
         scratch_shapes=[
@@ -315,8 +360,8 @@
             pltpu.VMEM((rank, width), bf16),
             pltpu.VMEM((rank, hidden), bf16),
             pltpu.VMEM((queries, flat), bf16),
-            pltpu.VMEM((n, part, 2 * rank), f32),
-            pltpu.VMEM((n, part, 2 * rank), f32),
+            pltpu.VMEM((ring, part, 2 * rank), f32),
+            pltpu.VMEM((ring, part, 2 * rank), f32),
             pltpu.VMEM((part, 2 * rank), f32),
             pltpu.VMEM((n, part, 2 * rank), f32),
             pltpu.VMEM((rank, 2 * rank), f32),
@@ -327,6 +372,7 @@
             dma((act_chunks + grad_chunks + 3,)),
             dma((4,)),
             dma((4,)),
+            dma((ring,)),
         ],
         compiler_params=pltpu.CompilerParams(
             collective_id=0, has_side_effects=True, vmem_limit_bytes=60 * 1024 * 1024

time: 37.6 us -> 33.7 us (0.90); the launches traced: 36.9 us -> 33.6 us
  Pallas kernels: 35.7 us -> 33 us
  other arithmetic: 1.24 us -> 0.56 us
    pallas_call x1, Pallas kernels: 35.7 us -> 33 us  [local(): pl.pallas_call(functools.partial(kernel, n), out_shape=pltpu.VMEM((exampl...]
    div x1, other arithmetic: 1.24 us -> 0.56 us  [local(): return total / jnp.sqrt(jnp.float32(flat * layers_all * length))]
where the time goes in v3:
time: 33.7 us; the launch traced here: 33.6 us
  Pallas kernels  33 us (98%)
  other arithmetic  0.56 us (2%)
    pallas_call x1, Pallas kernels, local(): pl.pallas_call(functools.partial(kernel, n), out_shape=pltpu.VMEM((exampl...  33 us

profile of v3, /device:TPU:2, one launch (start us, length us, event | category | flops | bytes accessed | tf_op | source)
XLA Modules:
  0.0 33.6 jit_solution(782246196815057897)
XLA Ops:
  0.0 33.0 %shard_map.55 = f32[2,64]{1,0:T(2,128)S(1)} custom-call(bf16[256,4096]{1,0:T(8,128)(2,1)} %bitcast.6, bf16[256,14336]{1,0:T(8,128)(2,1)} %bitcast.5, bf16[64,4096]{1,0:T(8,128)(2,1)} %bitcast.8, bf16[64,14336]{1,0:T(8,128)(2,1)} %bitcast.7, bf16[64,4096]{1,0:T(8,128)(2,1)} %bitcast.9), custom_call_target="tpu_custom_call" | custom-call | tf_op jit(solution)/shard_map/pallas_call | solution.py:352
  33.0 0.6 %broadcast_multiply_fusion = f32[2,64]{1,0:T(2,128)} fusion(f32[2,64]{1,0:T(2,128)S(1)} %shard_map.55), kind=kLoop, calls=%fused_computation | loop fusion | flops 128 | bytes 1024 | tf_op jit(solution)/shard_map/div | solution.py:388

commit v4 on v3

--- a/solution.py
+++ b/solution.py
@@ -11,7 +11,6 @@
 HIGHEST = lax.Precision.HIGHEST
 CHUNK = 2048
 PANEL = 8
-EARLY = 5
 NT = (((1,), (1,)), ((), ()))
 TN = (((0,), (0,)), ((), ()))
 
@@ -31,12 +30,10 @@
     lane_row = lax.rem(lanes((1, shape[1])), size)
     row8 = rows_of((8, shape[1]))
 
+    base = jnp.where(left, 0, size)
+
     def column(k):
-        return jnp.where(
-            left,
-            jnp.broadcast_to(a[:, k : k + 1], shape),
-            jnp.broadcast_to(a[:, size + k : size + k + 1], shape),
-        )
+        return jnp.take_along_axis(a, base + k, axis=1, mode="promise_in_bounds")
 
     def with_rows(x, k, first, second):
         at = k // 8 * 8
@@ -94,6 +91,29 @@
     wide = jnp.dot(pair[0], weights[0], preferred_element_type=jnp.float32)
     rest = jnp.dot(pair[1], weights[1], preferred_element_type=jnp.float32)
     return wide[:, :width] + (wide[:, width:] + rest)
+
+
+def by_part(pairs, weights):
+    return [product(pair, weights) for pair in pairs]
+
+
+def by_term(pairs, weights):
+    width = weights[1].shape[1]
+    wide = [jnp.dot(p[0], weights[0], preferred_element_type=jnp.float32) for p in pairs]
+    rest = [jnp.dot(p[1], weights[1], preferred_element_type=jnp.float32) for p in pairs]
+    return [w[:, :width] + (w[:, width:] + r) for w, r in zip(wide, rest)]
+
+
+def deep(pairs, weights):
+    width = weights[1].shape[1]
+    first = jnp.concatenate([weights[0][:, :width], weights[0][:, width:], weights[1]], axis=0)
+    return [
+        jnp.dot(
+            jnp.concatenate([p[0], p[0], p[1]], axis=1), first,
+            preferred_element_type=jnp.float32,
+        )
+        for p in pairs
+    ]
 
 
 def kernel(
@@ -203,7 +223,6 @@
     cov = jnp.where(left, total[:rank], total[rank:])
     for z in range(ring):
         cov_v[z] = cov[z * part : (z + 1) * part]
-    own_g[...] = jnp.where(left, pltpu.roll(grams[0][:rank], rank, 1), grams[1][:rank])
     pl.semaphore_wait(barrier, 3 * n - 1)
 
     def push(src, dst, send, recv, dp):
@@ -218,19 +237,35 @@
     def share(dz):
         push(own_g, g_v.at[i], send_sem.at[2], g_sem.at[place], member(0, dz)).start()
 
+    def block_from(dz):
+        return column * ring + lax.rem(place + ring - dz, ring)
+
+    def arrived(dz):
+        block = block_from(dz)
+        push(own_g, g_v.at[block], send_sem.at[2], g_sem.at[lax.rem(block, ring)], i).wait_recv()
+
+    def relay(dz, step):
+        block = block_from(dz)
+        for dh, sem in ((1, recv_sem.at[2]), (0, g_sem.at[lax.rem(block, ring)])):
+            push(
+                g_v.at[block], g_v.at[block], send_sem.at[2], sem, member(dh, step)
+            ).start()
+
     def forward(dz):
-        z = lax.rem(place + ring - dz, ring)
-        block = g_v.at[column * ring + z]
-        push(own_g, block, send_sem.at[2], g_sem.at[z], i).wait_recv()
-        push(block, block, send_sem.at[2], recv_sem.at[2], partner).start()
+        block = block_from(dz)
+        push(g_v.at[block], g_v.at[block], send_sem.at[2], recv_sem.at[2], partner).start()
+
+    direct = [dz for dz in far_first if min(dz, ring - dz) <= 2]
+    relayed = [dz for dz in far_first if dz not in direct][::-1]
 
     for dz in far_first:
         push(
             cov_v.at[lax.rem(place + dz, ring)], cov_r.at[place],
             send_sem.at[0], recv_sem.at[0], member(0, dz),
         ).start()
+    own_g[...] = jnp.where(left, pltpu.roll(grams[0][:rank], rank, 1), grams[1][:rank])
     push(own_g, g_v.at[i], send_sem.at[2], recv_sem.at[2], partner).start()
-    for dz in far_first[:EARLY]:
+    for dz in direct:
         share(dz)
     cov_r[place] = cov_v[place]
     g_v[i] = own_g[...]
@@ -242,9 +277,16 @@
     f_v[i] = piece
     for p in peers:
         push(piece_v, f_v.at[i], send_sem.at[1], recv_sem.at[1], p).start()
-    for dz in far_first[EARLY:]:
-        share(dz)
-    for dz in far_first:
+    if relayed:
+        arrived(2)
+        arrived(ring - 2)
+        relay(2, 1)
+        relay(ring - 2, ring - 1)
+        turn = 2 + (ring - 4) * lax.rem(l, 2)
+        relay(turn, turn)
+    for dz in direct:
+        if not relayed or min(dz, ring - dz) < 2:
+            arrived(dz)
         forward(dz)
     all_of(f_v, n - 1, recv_sem.at[1])
     f = jnp.concatenate([f_v[z] + f_v[ring + z] for z in range(ring)], axis=0)
@@ -264,28 +306,32 @@
     twice_out = standing(
         jnp.concatenate([jnp.where(left, turned, 0.0), jnp.where(left, 0.0, inv)], axis=0)
     )
+    for dz in relayed:
+        arrived(dz)
     all_of(g_v, ring, recv_sem.at[2])
     block = 2 * rank
     count = n // 2
-    g_rows = [
-        g_v[h * count : (h + 1) * count].reshape(count * rank, block) for h in range(2)
-    ]
-    halves = [product(moving(rows), twice_out) for rows in g_rows]
-    for h in range(2):
+    parts = min(4, n * rank // block)
+    size = n * rank // parts
+    g_rows = g_v[...].reshape(n * rank, block)
+    lifted = [moving(g_rows[h * size : (h + 1) * size]) for h in range(parts)]
+    halves = by_part(lifted, twice_out)
+    lifted = []
+    for h in range(parts):
         turned_rows = jnp.concatenate(
-            [halves[h][b * block : (b + 1) * block].T for b in range(count // 2)], axis=0
-        )
-        halves[h] = moving(turned_rows)
-    for h in range(2):
-        c_v[h * count * rank : (h + 1) * count * rank] = product(halves[h], twice_in)
+            [halves[h][b * block : (b + 1) * block].T for b in range(size // block)], axis=0
+        )
+        lifted.append(moving(turned_rows))
+    for h, c in enumerate(by_part(lifted, twice_in)):
+        c_v[h * size : (h + 1) * size] = c
     q_load.wait()
     in_left = lanes((n, 2 * rank)) < rank
+    by_output = jnp.swapaxes(c_v[...].reshape(n, rank, 2 * rank), 0, 1)
     scores = jnp.zeros((2 * n, q_v.shape[0]), jnp.float32)
     for o in range(0, rank, 4):
         firsts, seconds = [], []
         for o2 in (o, o + 2):
-            a = c_v[pl.ds(o2, n, stride=rank), :]
-            b = c_v[pl.ds(o2 + 1, n, stride=rank), :]
+            a, b = by_output[o2], by_output[o2 + 1]
             firsts.append(jnp.where(in_left, a, pltpu.roll(b, rank, 1)))
             seconds.append(jnp.where(in_left, pltpu.roll(a, rank, 1), b))
         flat = jnp.concatenate(
@@ -308,7 +354,7 @@
             device_id=(p, i), device_id_type=MESH,
         )
 
-    for p in range(n):
+    for p in peers + [i]:
         unless_self(p, lambda q: s_copy(q).start())
 
     @pl.when(i == l)

time: 33.7 us -> 32 us (0.950)
  Pallas kernels: 33 us -> 31.1 us
    pallas_call x1, Pallas kernels: 33 us -> 31.1 us  [local(): pl.pallas_call(functools.partial(kernel, n), out_shape=pltpu.VMEM((exampl...]
where the time goes in v4:
time: 32 us; the launch traced here: 31.7 us
  Pallas kernels  31.1 us (97%)
  other arithmetic  0.56 us (2%)
    pallas_call x1, Pallas kernels, local(): pl.pallas_call(functools.partial(kernel, n), out_shape=pltpu.VMEM((exampl...  31.1 us

profile of v4, /device:TPU:2, one launch (start us, length us, event | category | flops | bytes accessed | tf_op | source)
XLA Modules:
  0.0 31.7 jit_solution(18249377797934157918)
XLA Ops:
  0.0 31.1 %shard_map.55 = f32[2,64]{1,0:T(2,128)S(1)} custom-call(bf16[256,4096]{1,0:T(8,128)(2,1)} %bitcast.6, bf16[256,14336]{1,0:T(8,128)(2,1)} %bitcast.5, bf16[64,4096]{1,0:T(8,128)(2,1)} %bitcast.8, bf16[64,14336]{1,0:T(8,128)(2,1)} %bitcast.7, bf16[64,4096]{1,0:T(8,128)(2,1)} %bitcast.9), custom_call_target="tpu_custom_call" | custom-call | tf_op jit(solution)/shard_map/pallas_call | solution.py:398
  31.2 0.6 %broadcast_multiply_fusion = f32[2,64]{1,0:T(2,128)} fusion(f32[2,64]{1,0:T(2,128)S(1)} %shard_map.55), kind=kLoop, calls=%fused_computation | loop fusion | flops 128 | bytes 1024 | tf_op jit(solution)/shard_map/div | solution.py:434

commit v5 on v4

--- a/solution.py
+++ b/solution.py
@@ -9,7 +9,7 @@
 
 MESH = pl.DeviceIdType.MESH
 HIGHEST = lax.Precision.HIGHEST
-CHUNK = 2048
+CHUNK = 1024
 PANEL = 8
 NT = (((1,), (1,)), ((), ()))
 TN = (((0,), (0,)), ((), ()))
@@ -147,7 +147,8 @@
     l = lax.axis_index("layer")
     rank = 64
     ring = n // 2
-    part = rank // ring
+    line = max(2, ring // 2)
+    part = rank // line
     act_chunks, grad_chunks = acts_v.shape[0], grads_v.shape[0]
     column, place = i // ring, lax.rem(i, ring)
 
@@ -188,9 +189,9 @@
         greet(l, j)
         return 0
 
-    lax.fori_loop(0, n, greet_far, 0)
     for p in peers:
         greet(p, l)
+    lax.fori_loop(0, n, greet_far, 0)
     tokens = acts_v.shape[1]
     length = tokens // 2
 
@@ -221,7 +222,7 @@
     total = grams[0] + grams[1]
     left = lanes((rank, 2 * rank)) < rank
     cov = jnp.where(left, total[:rank], total[rank:])
-    for z in range(ring):
+    for z in range(line):
         cov_v[z] = cov[z * part : (z + 1) * part]
     pl.semaphore_wait(barrier, 3 * n - 1)
 
@@ -258,20 +259,22 @@
     direct = [dz for dz in far_first if min(dz, ring - dz) <= 2]
     relayed = [dz for dz in far_first if dz not in direct][::-1]
 
-    for dz in far_first:
+    seat = lax.rem(place, line)
+    for d in range(1, line):
+        other = lax.rem(seat + d, line)
         push(
-            cov_v.at[lax.rem(place + dz, ring)], cov_r.at[place],
-            send_sem.at[0], recv_sem.at[0], member(0, dz),
+            cov_v.at[other], cov_r.at[seat], send_sem.at[0], recv_sem.at[0],
+            i - seat + other,
         ).start()
     own_g[...] = jnp.where(left, pltpu.roll(grams[0][:rank], rank, 1), grams[1][:rank])
     push(own_g, g_v.at[i], send_sem.at[2], recv_sem.at[2], partner).start()
     for dz in direct:
         share(dz)
-    cov_r[place] = cov_v[place]
+    cov_r[seat] = cov_v[seat]
     g_v[i] = own_g[...]
-    all_of(cov_r, ring - 1, recv_sem.at[0])
+    all_of(cov_r, line - 1, recv_sem.at[0])
     piece = cov_r[0]
-    for z in range(1, ring):
+    for z in range(1, line):
         piece += cov_r[z]
     piece_v[...] = piece
     f_v[i] = piece
@@ -289,7 +292,9 @@
             arrived(dz)
         forward(dz)
     all_of(f_v, n - 1, recv_sem.at[1])
-    f = jnp.concatenate([f_v[z] + f_v[ring + z] for z in range(ring)], axis=0)
+    f = jnp.concatenate(
+        [sum(f_v[p] for p in range(z + line, n, line)) + f_v[z] for z in range(line)], axis=0
+    )
     f = f / jnp.float32(tokens * n)
     on_diagonal = lax.rem(lanes(f.shape), rank) == rows_of(f.shape)
     diagonal = jnp.sum(jnp.where(on_diagonal, f, 0.0), axis=0, keepdims=True)
@@ -361,7 +366,7 @@
     def _():
         s_r[l] = s_v[i]
 
-    all_of(cov_r, ring - 1, send_sem.at[0])
+    all_of(cov_r, line - 1, send_sem.at[0])
     all_of(f_v, n - 1, send_sem.at[1])
     all_of(g_v, n - 1, send_sem.at[2])
 
@@ -390,7 +395,8 @@
     queries, flat = query_grads.shape[1:]
     tokens = examples * length
     ring = n // 2
-    part = rank // ring
+    line = max(2, ring // 2)
+    part = rank // line
     f32, bf16 = jnp.float32, jnp.bfloat16
     dma = pltpu.SemaphoreType.DMA
     act_chunks, grad_chunks = width // CHUNK, hidden // CHUNK
@@ -406,8 +412,8 @@
             pltpu.VMEM((rank, width), bf16),
             pltpu.VMEM((rank, hidden), bf16),
             pltpu.VMEM((queries, flat), bf16),
-            pltpu.VMEM((ring, part, 2 * rank), f32),
-            pltpu.VMEM((ring, part, 2 * rank), f32),
+            pltpu.VMEM((line, part, 2 * rank), f32),
+            pltpu.VMEM((line, part, 2 * rank), f32),
             pltpu.VMEM((part, 2 * rank), f32),
             pltpu.VMEM((n, part, 2 * rank), f32),
             pltpu.VMEM((rank, 2 * rank), f32),

time: 32 us -> 31.6 us (0.988)
  Pallas kernels: 31.1 us -> 30.5 us
    pallas_call x1, Pallas kernels: 31.1 us -> 30.5 us  [local(): pl.pallas_call(functools.partial(kernel, n), out_shape=pltpu.VMEM((exampl...]
where the time goes in v5:
time: 31.6 us; the launch traced here: 31.1 us
  Pallas kernels  30.5 us (97%)
  other arithmetic  0.56 us (2%)
    pallas_call x1, Pallas kernels, local(): pl.pallas_call(functools.partial(kernel, n), out_shape=pltpu.VMEM((exampl...  30.5 us

profile of v5, /device:TPU:2, one launch (start us, length us, event | category | flops | bytes accessed | tf_op | source)
XLA Modules:
  0.0 31.1 jit_solution(5103647154026657779)
XLA Ops:
  0.0 30.5 %shard_map.55 = f32[2,64]{1,0:T(2,128)S(1)} custom-call(bf16[256,4096]{1,0:T(8,128)(2,1)} %bitcast.6, bf16[256,14336]{1,0:T(8,128)(2,1)} %bitcast.5, bf16[64,4096]{1,0:T(8,128)(2,1)} %bitcast.8, bf16[64,14336]{1,0:T(8,128)(2,1)} %bitcast.7, bf16[64,4096]{1,0:T(8,128)(2,1)} %bitcast.9), custom_call_target="tpu_custom_call" | custom-call | tf_op jit(solution)/shard_map/pallas_call | solution.py:404
  30.5 0.6 %broadcast_multiply_fusion = f32[2,64]{1,0:T(2,128)} fusion(f32[2,64]{1,0:T(2,128)S(1)} %shard_map.55), kind=kLoop, calls=%fused_computation | loop fusion | flops 128 | bytes 1024 | tf_op jit(solution)/shard_map/div | solution.py:440

commit v6 on v5

--- a/solution.py
+++ b/solution.py
@@ -256,7 +256,8 @@
         block = block_from(dz)
         push(g_v.at[block], g_v.at[block], send_sem.at[2], recv_sem.at[2], partner).start()
 
-    direct = [dz for dz in far_first if min(dz, ring - dz) <= 2]
+    direct = [dz for dz in far_first if min(dz, ring - dz) <= 3]
+    direct.sort(key=lambda dz: (2, 0, 1)[min(dz, ring - dz) - 1])
     relayed = [dz for dz in far_first if dz not in direct][::-1]
 
     seat = lax.rem(place, line)
@@ -283,12 +284,10 @@
     if relayed:
         arrived(2)
         arrived(ring - 2)
-        relay(2, 1)
-        relay(ring - 2, ring - 1)
         turn = 2 + (ring - 4) * lax.rem(l, 2)
         relay(turn, turn)
     for dz in direct:
-        if not relayed or min(dz, ring - dz) < 2:
+        if not relayed or min(dz, ring - dz) != 2:
             arrived(dz)
         forward(dz)
     all_of(f_v, n - 1, recv_sem.at[1])

time: 31.6 us -> 33.4 us (1.057); the launches traced: 31.1 us -> 33.3 us
  Pallas kernels: 30.5 us -> 32.7 us
    pallas_call x1, Pallas kernels: 30.5 us -> 32.7 us  [local(): pl.pallas_call(functools.partial(kernel, n), out_shape=pltpu.VMEM((exampl...]
where the time goes in v6:
time: 33.4 us; the launch traced here: 33.3 us
  Pallas kernels  32.7 us (98%)
  other arithmetic  0.56 us (2%)
    pallas_call x1, Pallas kernels, local(): pl.pallas_call(functools.partial(kernel, n), out_shape=pltpu.VMEM((exampl...  32.7 us

profile of v6, /device:TPU:2, one launch (start us, length us, event | category | flops | bytes accessed | tf_op | source)
XLA Modules:
  0.0 33.3 jit_solution(10633913461012676116)
XLA Ops:
  0.0 32.7 %shard_map.55 = f32[2,64]{1,0:T(2,128)S(1)} custom-call(bf16[256,4096]{1,0:T(8,128)(2,1)} %bitcast.6, bf16[256,14336]{1,0:T(8,128)(2,1)} %bitcast.5, bf16[64,4096]{1,0:T(8,128)(2,1)} %bitcast.8, bf16[64,14336]{1,0:T(8,128)(2,1)} %bitcast.7, bf16[64,4096]{1,0:T(8,128)(2,1)} %bitcast.9), custom_call_target="tpu_custom_call" | custom-call | tf_op jit(solution)/shard_map/pallas_call | solution.py:403
  32.7 0.6 %broadcast_multiply_fusion = f32[2,64]{1,0:T(2,128)} fusion(f32[2,64]{1,0:T(2,128)S(1)} %shard_map.55), kind=kLoop, calls=%fused_computation | loop fusion | flops 128 | bytes 1024 | tf_op jit(solution)/shard_map/div | solution.py:439
